TPU v7x, 32 devices: a whole 2x2x4 slice. The times are simulated.
32 devices in a mesh: row: 8 (over y, x, core), col: 4 (over z).
Axes of the slice: x: 2, y: 2, z: 4, core: 2. Of those that a mesh axis runs over, the one named last changes fastest.
Arguments:
- alignment_state: bfloat16 [128, 128, 256], P('col', 'row'), may hold values from -6 to 6
- layer_norm_gain: float32 [256], replicated, may hold values from 0.1 to 1.9
- left_weight_matrix: bfloat16 [256, 32], replicated, may hold values from -0.375 to 0.375
- right_weight_matrix: bfloat16 [256, 32], replicated, may hold values from -0.375 to 0.375
- output_weight_matrix: bfloat16 [1024, 128], replicated, may hold values from -0.1875 to 0.1875
- output_bias_vector: float32 [128], replicated, may hold values from -3 to 3
- pair_update_cotangent: bfloat16 [128, 128, 128], P('row', 'col'), may hold values from -40 to 40
Outputs:
- pair_update_output: bfloat16 [128, 128, 128], P('row', 'col')
- alignment_gradient: bfloat16 [128, 128, 256], P('col', 'row')
- left_weight_gradient: float32 [256, 32], replicated
- right_weight_gradient: float32 [256, 32], replicated
- out_w_grad: float32 [1024, 128], P(('row', 'col'))
- norm_gain_gradient: float32 [256], replicated
- output_bias_gradient: float32 [128], replicated
All inputs are finite; a program needn't handle non-finite values.
Results may differ from a plain program's by a relative error of at most 0.024.
Values may be sent and summed in bfloat16 or wider, within the bound.
No kernel may reach another device: no remote copies, remote signals or barrier semaphores. Data moves between devices by JAX's collectives and lax.ppermute only.
A program may use at most 64 MiB of HBM per device.

v0:
```python
import jax
import jax.numpy as jnp
from jax import lax
from jax.sharding import PartitionSpec as P


def from_root(block, axis, holder):
    block = jnp.where(lax.axis_index(axis) == holder, block, jnp.zeros_like(block))
    return lax.psum(block, axis)


def apply_layer_norm(alignment_state):
    value_entries = alignment_state.astype(jnp.float32)
    center = value_entries - jnp.mean(value_entries, axis=-1, keepdims=True)
    inverse_deviation = lax.rsqrt(jnp.mean(center * center, axis=-1, keepdims=True) + 1e-05)
    return (center * inverse_deviation, inverse_deviation)


def on_device(
    alignment_state,
    layer_norm_gain,
    left_weight_matrix,
    right_weight_matrix,
    output_weight_matrix,
    output_bias_vector,
    pair_update_cotangent,
):
    sequence_block_local, residue_block_local, alignment_weight = alignment_state.shape
    proj_w = left_weight_matrix.shape[1]
    pair_w = output_weight_matrix.shape[1]
    row_count = lax.axis_size("row")
    col_count = lax.axis_size("col")
    row_ratio = row_count // col_count
    total_res = residue_block_local * row_count
    col_res = residue_block_local * row_ratio
    col_index = lax.axis_index("col")
    row_index = lax.axis_index("row")
    normed_alignment, inverse_deviation = apply_layer_norm(alignment_state)
    layer_norm_output = (normed_alignment * layer_norm_gain).astype(jnp.bfloat16)
    normed_flat_rows = layer_norm_output.reshape(-1, alignment_weight)
    left_local = (
        jnp.dot(normed_flat_rows, left_weight_matrix, preferred_element_type=jnp.float32)
        .astype(jnp.bfloat16)
        .reshape(sequence_block_local, residue_block_local, proj_w)
    )
    right_local = (
        jnp.dot(normed_flat_rows, right_weight_matrix, preferred_element_type=jnp.float32)
        .astype(jnp.bfloat16)
        .reshape(sequence_block_local, residue_block_local, proj_w)
    )
    left_all, right_rows = (
        lax.all_gather(left_local, "col", axis=0, tiled=True),
        lax.all_gather(right_local, "col", axis=0, tiled=True),
    )
    seq_total = left_all.shape[0]
    right_every = lax.all_gather(right_rows, "row", axis=1, tiled=True)
    right_block = lax.dynamic_slice_in_dim(right_every, col_index * col_res, col_res, 1)
    block_res = min(8, residue_block_local)

    def visit(totals, row_start):
        right_acc, projection_running_sum = totals
        left_part = lax.dynamic_slice_in_dim(left_all, row_start, block_res, 1)
        cot_part = lax.dynamic_slice_in_dim(pair_update_cotangent, row_start, block_res, 0)
        outer_prod = jnp.einsum(
            "sic,sjd->ijcd", left_part, right_block, preferred_element_type=jnp.float32
        )
        outer_flat = (
            (outer_prod / seq_total)
            .astype(jnp.bfloat16)
            .reshape(block_res * col_res, proj_w * proj_w)
        )
        cot_flat = cot_part.reshape(block_res * col_res, pair_w)
        pair_part = (
            jnp.dot(outer_flat, output_weight_matrix, preferred_element_type=jnp.float32)
            + output_bias_vector
        ).astype(jnp.bfloat16)
        projection_running_sum = projection_running_sum + lax.dot_general(
            outer_flat, cot_flat, (((0,), (0,)), ((), ())), preferred_element_type=jnp.float32
        )
        outer_grad = lax.dot_general(
            cot_flat,
            output_weight_matrix,
            (((1,), (1,)), ((), ())),
            preferred_element_type=jnp.float32,
        ).astype(jnp.bfloat16)
        outer_grad = outer_grad.reshape(block_res, col_res, proj_w, proj_w)
        left_part_grad = (
            jnp.einsum("ijcd,sjd->sic", outer_grad, right_block, preferred_element_type=jnp.float32)
            / seq_total
        )
        right_acc = (
            right_acc
            + jnp.einsum("ijcd,sic->sjd", outer_grad, left_part, preferred_element_type=jnp.float32)
            / seq_total
        )
        return (
            (right_acc, projection_running_sum),
            (pair_part.reshape(block_res, col_res, pair_w), left_part_grad),
        )

    starts = jnp.arange(residue_block_local // block_res, dtype=jnp.int32) * block_res
    initial = (
        jnp.zeros((seq_total, col_res, proj_w), jnp.float32),
        jnp.zeros((proj_w * proj_w, pair_w), jnp.float32),
    )
    (right_acc, projection_running_sum), (pair_parts, left_parts) = lax.scan(visit, initial, starts)
    pair_update_output = pair_parts.reshape(residue_block_local, col_res, pair_w)
    left_partial = jnp.transpose(left_parts, (1, 0, 2, 3)).reshape(
        seq_total, residue_block_local, proj_w
    )
    left_d = lax.psum_scatter(
        left_partial.astype(jnp.bfloat16), "col", scatter_dimension=0, tiled=True
    )
    right_full = lax.psum(right_acc.astype(jnp.bfloat16), "row").astype(jnp.float32)
    right_half = lax.dynamic_slice_in_dim(
        right_full, row_index % row_ratio * residue_block_local, residue_block_local, 1
    )
    right_home = from_root(right_half.astype(jnp.bfloat16), "col", row_index // row_ratio).astype(
        right_half.dtype
    )
    right_d = lax.dynamic_slice_in_dim(
        right_home, col_index * sequence_block_local, sequence_block_local, 0
    ).astype(jnp.bfloat16)
    left_flat = left_d.reshape(-1, proj_w)
    right_flat = right_d.reshape(-1, proj_w)
    normed_derivative = lax.dot_general(
        left_flat, left_weight_matrix, (((1,), (1,)), ((), ())), preferred_element_type=jnp.float32
    )
    normed_derivative = normed_derivative + lax.dot_general(
        right_flat,
        right_weight_matrix,
        (((1,), (1,)), ((), ())),
        preferred_element_type=jnp.float32,
    )
    normed_derivative = normed_derivative.reshape(
        sequence_block_local, residue_block_local, alignment_weight
    )
    scaled_product = normed_derivative * layer_norm_gain
    alignment_gradient = (
        (
            scaled_product
            - jnp.mean(scaled_product, axis=-1, keepdims=True)
            - normed_alignment * jnp.mean(scaled_product * normed_alignment, axis=-1, keepdims=True)
        )
        * inverse_deviation
    ).astype(jnp.bfloat16)
    weight_left = lax.dot_general(
        normed_flat_rows, left_flat, (((0,), (0,)), ((), ())), preferred_element_type=jnp.float32
    )
    weight_right = lax.dot_general(
        normed_flat_rows, right_flat, (((0,), (0,)), ((), ())), preferred_element_type=jnp.float32
    )
    gain_part = jnp.sum(normed_derivative * normed_alignment, axis=(0, 1))
    bias_part = jnp.sum(pair_update_cotangent, axis=(0, 1), dtype=jnp.float32)
    param_totals = lax.psum((weight_left, weight_right, gain_part, bias_part), ("row", "col"))
    proj_partial = lax.psum_scatter(
        projection_running_sum.astype(jnp.bfloat16), "row", scatter_dimension=0, tiled=True
    ).astype(jnp.float32)
    proj_total = lax.psum_scatter(proj_partial, "col", scatter_dimension=0, tiled=True)
    return (
        pair_update_output,
        alignment_gradient,
        param_totals[0] / total_res,
        param_totals[1] / total_res,
        proj_total / total_res,
        param_totals[2] / total_res,
        param_totals[3] / total_res,
    )


def solution(mesh):
    return jax.shard_map(
        on_device,
        mesh=mesh,
        in_specs=(P("col", "row", None), P(), P(), P(), P(), P(), P("row", "col", None)),
        out_specs=(
            P("row", "col", None),
            P("col", "row", None),
            P(),
            P(),
            P(("row", "col"), None),
            P(),
            P(),
        ),
        check_vma=False,
    )
```

profile of v0, /device:TPU:0, one launch (start us, length us, event | category | flops | bytes accessed | tf_op | source)
XLA Modules:
  0.0 416.1 jit_solution(7871246451103388164)
XLA Ops:
  7.2 1.1 convert_reduce_fusion
  8.4 1.2 fusion.27
  9.6 1.2 fusion.21
  10.8 0.2 convolution_convert_fusion.1
  11.0 0.1 copy.42
  11.1 18.0 %all_gather.10 = bf16[128,16,32]{2,1,0:T(8,128)(2,1)} all-gather(bf16[32,16,32]{2,1,0:T(8,128)(2,1)S(1)} %bitcast.126), channel_id=1, replica_groups=mesh['row'=8,'col'=4] {'col'}, dimensions={0}, use_global_device_ids=true | all-gather | bytes 163840 | tf_op jit(solution)/shard_map/all_gather | solution.py:53
  29.2 0.2 convolution_convert_fusion.2
  29.4 0.1 copy.41
  29.6 16.3 %all_gather.9 = bf16[128,16,32]{2,1,0:T(8,128)(2,1)S(1)} all-gather(bf16[32,16,32]{2,1,0:T(8,128)(2,1)S(1)} %bitcast.127), channel_id=1, replica_groups=mesh['row'=8,'col'=4] {'col'}, dimensions={0}, use_global_device_ids=true | all-gather | bytes 163840 | tf_op jit(solution)/shard_map/all_gather | solution.py:52
  45.9 0.4 copy.43
  46.3 0.5 iota_multiply_fusion
  46.8 21.7 %all-gather.2.cloned.1.call-done = bf16[128,128,32]{2,1,0:T(8,128)(2,1)} async-done(((bf16[128,16,32]{2,1,0:T(8,128)(2,1)}), bf16[128,128,32]{2,1,0:T(8,128)(2,1)}) %all-gather.2.cloned.1.call-update) | async-done | bytes 1048592 | tf_op jit(solution)/shard_map/all_gather | solution.py:56
  68.5 1.3 constant_dynamic-slice_fusion.1
  69.8 1.8 copy.44
  71.6 32.6 %while.17 = (s32[]{:T(128)}, f32[128,32,32]{0,2,1:T(8,128)}, f32[1024,128]{1,0:T(8,128)S(1)}, bf16[2,8,32,128]{3,2,1,0:T(8,128)(2,1)}, bf16[2,128,8,32]{1,3,2,0:...) while((s32[]{:T(128)}, f32[128,32,32]{0,2,1:T(8,128)}, ...), condition=%wide.region_3.4_spmd.clone, body=%wide.region_2.3_spmd.clone.sunk | while | flops 404193280 | bytes 15928666 | solution.py:106
  71.6 1.2 dynamic_slice.46
  74.8 1.7 fusion.79
  76.5 2.2 reshape.95
  78.7 0.9 constant_dynamic-slice_fusion.3
  79.5 0.5 convolution_add_fusion.4
  80.0 0.8 copy-done.2
  80.8 0.3 convolution_convert_fusion.4
  81.1 1.6 reshape.94
  82.7 1.5 fusion.78
  84.3 0.3 fusion.80
  84.6 0.6 copy-done.17
  85.3 2.1 fusion.81
  87.4 1.2 dynamic_slice.46
  90.6 1.7 fusion.79
  92.2 2.2 reshape.95
  94.5 0.9 constant_dynamic-slice_fusion.3
  95.3 0.5 convolution_add_fusion.4
  95.8 0.8 copy-done.2
  96.6 0.3 convolution_convert_fusion.4
  96.9 1.6 reshape.94
  98.5 2.6 fusion.78
  101.1 0.3 fusion.80
  101.5 0.6 copy-done.17
  102.1 2.1 fusion.81
  104.3 1.8 convert_element_type.67
  106.2 2.1 copy.45
  108.4 0.6 convert_reduce_fusion.1
  109.0 51.2 %all-reduce.5.cloned.1.call-done = bf16[128,32,32]{0,2,1:T(8,128)(2,1)} async-done(((bf16[128,32,32]{0,2,1:T(8,128)(2,1)}), bf16[128,32,32]{0,2,1:T(8,128)(2,1)}) %all-reduce.5.cloned.1.call-update) | async-done | bytes 262160 | tf_op jit(solution)/shard_map/psum | solution.py:114
  160.2 1.6 fusion.28
  161.8 21.9 %reduce-scatter.4.cloned.1.call-done = bf16[32,16,32]{2,1,0:T(8,128)(2,1)} async-done(((bf16[128,16,32]{2,1,0:T(8,128)(2,1)}), bf16[32,16,32]{2,1,0:T(8,128)(2,1)}) %reduce-scatter.4.cloned.1.call-update) | async-done | bytes 32784 | tf_op jit(solution)/shard_map/reduce_scatter | solution.py:111
  183.7 1.1 fusion.29
  184.8 1.7 convolution_bitcast_fusion.3
  186.5 32.9 %all-reduce.7.cloned.1.call-done = bf16[128,16,32]{0,2,1:T(8,128)(2,1)} async-done(((bf16[128,16,32]{0,2,1:T(8,128)(2,1)}), bf16[128,16,32]{0,2,1:T(8,128)(2,1)}) %all-reduce.7.cloned.1.call-update) | async-done | bytes 131088 | tf_op jit(solution)/shard_map/psum | solution.py:9
  219.4 1.0 convert_convert_fusion
  220.4 0.2 copy.46
  220.6 0.8 convolution_bitcast_fusion.2
  221.4 0.3 multiply_reduce_fusion
  221.7 0.8 fusion.26
  222.6 0.7 convert_element_type.73
  223.4 0.1 div.63
  223.5 1.0 fusion.25
  224.5 122.1 %all-reduce.9.cloned.1.call-done = (f32[256,32]{0,1:T(8,128)}, f32[256,32]{0,1:T(8,128)}, f32[256]{0:T(256)}, f32[128]{0:T(128)}) async-done(((f32[256,32]{0,1:T(8,128)}, f32[256,32]{0,1:T(8,128)}, f32[256]{0:T(256)}, f32[128]{0:T(128)}), (f32[256,32]{0,1:T(8,128)}, f32[256,32]{0,1:T(8,128)}, f32[256]{0:T(256)}, f32[128]{0:T(128)})) %all-reduce.9.cloned.1.call-update) | async-done | bytes 67088 | tf_op jit(solution)/shard_map/psum | solution.py:155
  346.7 1.2 broadcast_multiply_fusion.6
  347.9 1.4 broadcast_multiply_fusion
  349.3 37.1 %reduce-scatter.6.cloned.1.call-done = bf16[128,128]{1,0:T(8,128)(2,1)} async-done(((bf16[1024,128]{1,0:T(8,128)(2,1)}), bf16[128,128]{1,0:T(8,128)(2,1)}) %reduce-scatter.6.cloned.1.call-update) | async-done | bytes 32784 | tf_op jit(solution)/shard_map/reduce_scatter | solution.py:156
  386.4 1.4 convert_element_type.74
  387.8 1.1 broadcast_multiply_fusion.7
  388.9 19.1 %reduce-scatter.8.cloned.1.call-done = f32[32,128]{1,0:T(8,128)} async-done(((f32[128,128]{1,0:T(8,128)}), f32[32,128]{1,0:T(8,128)}) %reduce-scatter.8.cloned.1.call-update) | async-done | bytes 16400 | tf_op jit(solution)/shard_map/reduce_scatter | solution.py:159
  408.0 1.3 broadcast_multiply_fusion.2
  (66 shorter events, 0.6 us)
Async XLA Ops:
  7.2 3.6 copy-start
  7.2 22.1 %copy-start.12 = (bf16[256,32]{0,1:T(8,128)(2,1)S(1)}, bf16[256,32]{0,1:T(8,128)(2,1)}, u32[]{:S(2)}) copy-start(bf16[256,32]{0,1:T(8,128)(2,1)} %param.11) | copy-start | bytes 49156
  7.2 61.3 %all-gather.2.cloned.1.call-start = ((), (), s32[]{:S(2)}) async-start(), calls=%async_computation.3 | async-start | bytes 4718592 | tf_op jit(solution)/shard_map/all_gather | solution.py:56
  8.3 2.4 copy-start.8
  9.6 1.2 copy-start.10
  10.8 18.8 %copy-start.5 = (bf16[32,16,256]{2,1,0:T(8,128)(2,1)}, bf16[32,16,256]{2,1,0:T(8,128)(2,1)S(1)}, u32[]{:S(2)}) copy-start(bf16[32,16,256]{2,1,0:T(8,128)(2,1)S(1)} %fusion.21) | copy-start | bytes 786436
  29.1 131.0 %all-reduce.5.cloned.1.call-start = ((), (), s32[]{:S(2)}) async-start(), calls=%async_computation.5 | async-start | bytes 524288 | tf_op jit(solution)/shard_map/psum | solution.py:114
  45.9 25.7 %copy-start.1 = (bf16[1024,128]{1,0:T(8,128)(2,1)S(1)}, bf16[1024,128]{1,0:T(8,128)(2,1)}, u32[]{:S(2)}) copy-start(bf16[1024,128]{1,0:T(8,128)(2,1)} %param.13) | copy-start | bytes 786436
  80.0 0.8 copy-start.2
  82.7 1.6 copy-start.15
  82.7 1.9 copy-start.16
  84.3 3.1 copy-start.3
  84.6 0.7 copy-start.17
  95.8 0.8 copy-start.2
  98.5 2.7 copy-start.15
  98.5 2.9 copy-start.16
  101.1 3.1 copy-start.3
  101.5 0.7 copy-start.17
  104.2 4.1 copy-start.7
  104.2 79.5 %copy-start.13 = (bf16[256,32]{0,1:T(8,128)(2,1)S(1)}, bf16[256,32]{0,1:T(8,128)(2,1)}, u32[]{:S(2)}) copy-start(bf16[256,32]{0,1:T(8,128)(2,1)} %param.11) | copy-start | bytes 49156
  104.2 80.6 %copy-start.6 = (bf16[32,16,256]{2,1,0:T(8,128)(2,1)S(1)}, bf16[32,16,256]{2,1,0:T(8,128)(2,1)}, u32[]{:S(2)}) copy-start(bf16[32,16,256]{2,1,0:T(8,128)(2,1)} %copy-done.5) | copy-start | bytes 786436
  106.1 115.3 %copy-start.14 = (f32[256]{0:T(256)S(1)}, f32[256]{0:T(256)}, u32[]{:S(2)}) copy-start(f32[256]{0:T(256)} %param.10) | copy-start | bytes 3076
  106.1 77.6 %reduce-scatter.4.cloned.1.call-start = ((), (), s32[]{:S(2)}) async-start(), calls=%async_computation.4 | async-start | bytes 655360 | tf_op jit(solution)/shard_map/reduce_scatter | solution.py:111
  108.3 113.5 %copy-start.4 = (bf16[32,16,256]{2,1,0:T(8,128)(2,1)S(1)}, bf16[32,16,256]{2,1,0:T(8,128)(2,1)}, u32[]{:S(2)}) copy-start(bf16[32,16,256]{2,1,0:T(8,128)(2,1)} %param.9) | copy-start | bytes 786436
  108.3 113.5 %copy-start.9 = (f32[32,16]{1,0:T(8,128)S(1)}, f32[32,16]{1,0:T(8,128)}, u32[]{:S(2)}) copy-start(f32[32,16]{1,0:T(8,128)} %copy-done.8) | copy-start | bytes 6148
  108.3 113.5 %copy-start.11 = (f32[32,16]{1,0:T(8,128)S(1)}, f32[32,16]{1,0:T(8,128)}, u32[]{:S(2)}) copy-start(f32[32,16]{1,0:T(8,128)} %copy-done.10) | copy-start | bytes 6148
  108.3 111.1 %all-reduce.7.cloned.1.call-start = ((), (), s32[]{:S(2)}) async-start(), calls=%async_computation.6 | async-start | bytes 262144 | tf_op jit(solution)/shard_map/psum | solution.py:9
  161.8 184.9 %all-reduce.9.cloned.1.call-start = ((), (), s32[]{:S(2)}) async-start(), calls=%async_computation.9 | async-start | bytes 134144 | tf_op jit(solution)/shard_map/psum | solution.py:155
  222.5 163.9 %reduce-scatter.6.cloned.1.call-start = ((), (), s32[]{:S(2)}) async-start(), calls=%async_computation.7 | async-start | bytes 294912 | tf_op jit(solution)/shard_map/reduce_scatter | solution.py:156
  223.3 184.6 %reduce-scatter.8.cloned.1.call-start = ((), (), s32[]{:S(2)}) async-start(), calls=%async_computation.8 | async-start | bytes 81920 | tf_op jit(solution)/shard_map/reduce_scatter | solution.py:159
Sparse Core Ops, SparseCore 0:
  29.3 39.2 all-gather.1
  106.2 53.8 all-reduce.4
  162.4 21.2 reduce-scatter.3
  186.5 32.8 all-reduce.6
  225.9 120.6 all-reduce.8
  349.5 36.8 reduce-scatter.5
  388.6 19.2 reduce-scatter.7
where the time goes:
time: 417 us; the launch traced here: 416 us
  waiting for transfers between devices  306 us (73%)
  blocking collectives  34.3 us (8%)
  local copies, waits for them, and re-layouts  21 us (5%)
  matrix products  18.1 us (4%)
  other arithmetic  18 us (4%)
  between operations  14.4 us (3%)
    psum x1, waiting for transfers between devices, on_device(): lax.psum((weight_left, weight_right, gain_part, bias_part), ('row', 'col'))  122 us
    psum x1, waiting for transfers between devices, on_device(): lax.psum(right_acc.astype(jnp.bfloat16), 'row').astype(jnp.float32)  51.2 us
    reduce_scatter x1, waiting for transfers between devices, on_device(): lax.psum_scatter(projection_running_sum.astype(jnp.bfloat16), 'row', scat...  37.1 us
    psum x1, waiting for transfers between devices, from_root(): return lax.psum(block, axis)  32.9 us
    reduce_scatter x1, waiting for transfers between devices, on_device(): lax.psum_scatter(left_partial.astype(jnp.bfloat16), 'col', scatter_dimens...  21.9 us
    all_gather x1, waiting for transfers between devices, on_device(): right_every = lax.all_gather(right_rows, 'row', axis=1, tiled=True)  21.7 us
    reduce_scatter x1, waiting for transfers between devices, on_device(): lax.psum_scatter(proj_partial, 'col', scatter_dimension=0, tiled=True)  19.1 us
    all_gather x1, blocking collectives, on_device(): lax.all_gather(right_local, 'col', axis=0, tiled=True)  18 us
  transfers between devices with their start and end apart: 7, of which 7 were waited for; matrix products, arithmetic and copies ran while one was open for 3% of the time, Pallas kernels for 0%

commit v1 on v0

--- a/solution.py
+++ b/solution.py
@@ -152,7 +152,9 @@
     )
     gain_part = jnp.sum(normed_derivative * normed_alignment, axis=(0, 1))
     bias_part = jnp.sum(pair_update_cotangent, axis=(0, 1), dtype=jnp.float32)
-    param_totals = lax.psum((weight_left, weight_right, gain_part, bias_part), ("row", "col"))
+    param_totals = lax.psum(
+        lax.psum((weight_left, weight_right, gain_part, bias_part), "row"), "col"
+    )
     proj_partial = lax.psum_scatter(
         projection_running_sum.astype(jnp.bfloat16), "row", scatter_dimension=0, tiled=True
     ).astype(jnp.float32)

time: 417 us -> 379 us (0.909)
  waiting for transfers between devices: 306 us -> 268 us
    psum x1 -> x2, waiting for transfers between devices: 122 us -> 87.6 us  [the longest x1 51.4 us: on_device(): lax.psum((weight_left, weight_right, gain_part, bias_part), 'row')]
  transfers between devices with their start and end apart: 7 -> 8, of which waited for: 7 -> 8; matrix products, arithmetic and copies ran while one was open for 3% -> 4% of each run, Pallas kernels for 0% -> 0%
where the time goes in v1:
time: 379 us
  waiting for transfers between devices  268 us (71%)
  blocking collectives  34.3 us (9%)
  local copies, waits for them, and re-layouts  20.9 us (6%)
  matrix products  18.1 us (5%)
  other arithmetic  18 us (5%)
  between operations  14.4 us (4%)
  loops' own time  4.07 us (1%)
    psum x1, waiting for transfers between devices, on_device(): lax.psum((weight_left, weight_right, gain_part, bias_part), 'row')  51.4 us
    psum x1, waiting for transfers between devices, on_device(): lax.psum(right_acc.astype(jnp.bfloat16), 'row').astype(jnp.float32)  51.2 us
    psum x1, waiting for transfers between devices, on_device(): lax.psum(lax.psum((weight_left, weight_right, gain_part, bias_part), 'row...  36.1 us
    reduce_scatter x1, waiting for transfers between devices, on_device(): lax.psum_scatter(projection_running_sum.astype(jnp.bfloat16), 'row', scat...  34.1 us
    psum x1, waiting for transfers between devices, from_root(): return lax.psum(block, axis)  32.9 us
    reduce_scatter x1, waiting for transfers between devices, on_device(): lax.psum_scatter(left_partial.astype(jnp.bfloat16), 'col', scatter_dimens...  21.9 us
    all_gather x1, waiting for transfers between devices, on_device(): right_every = lax.all_gather(right_rows, 'row', axis=1, tiled=True)  21.7 us
    reduce_scatter x1, waiting for transfers between devices, on_device(): lax.psum_scatter(proj_partial, 'col', scatter_dimension=0, tiled=True)  19 us
  transfers between devices with their start and end apart: 8, of which 8 were waited for; matrix products, arithmetic and copies ran while one was open for 4% of the time, Pallas kernels for 0%

profile of v1, /device:TPU:0, one launch (start us, length us, event | category | flops | bytes accessed | tf_op | source)
XLA Modules:
  0.0 378.6 jit_solution(17549846217125612770)
XLA Ops:
  7.2 1.1 convert_reduce_fusion
  8.4 1.2 fusion.27
  9.6 1.2 fusion.21
  10.8 0.2 convolution_convert_fusion.1
  11.0 0.1 copy.42
  11.1 18.0 %all_gather.10 = bf16[128,16,32]{2,1,0:T(8,128)(2,1)} all-gather(bf16[32,16,32]{2,1,0:T(8,128)(2,1)S(1)} %bitcast.126), channel_id=1, replica_groups=mesh['row'=8,'col'=4] {'col'}, dimensions={0}, use_global_device_ids=true | all-gather | bytes 163840 | tf_op jit(solution)/shard_map/all_gather | solution.py:53
  29.2 0.2 convolution_convert_fusion.2
  29.4 0.1 copy.41
  29.6 16.3 %all_gather.9 = bf16[128,16,32]{2,1,0:T(8,128)(2,1)S(1)} all-gather(bf16[32,16,32]{2,1,0:T(8,128)(2,1)S(1)} %bitcast.127), channel_id=1, replica_groups=mesh['row'=8,'col'=4] {'col'}, dimensions={0}, use_global_device_ids=true | all-gather | bytes 163840 | tf_op jit(solution)/shard_map/all_gather | solution.py:52
  45.9 0.4 copy.43
  46.3 0.5 iota_multiply_fusion
  46.8 21.7 %all-gather.2.cloned.1.call-done = bf16[128,128,32]{2,1,0:T(8,128)(2,1)} async-done(((bf16[128,16,32]{2,1,0:T(8,128)(2,1)}), bf16[128,128,32]{2,1,0:T(8,128)(2,1)}) %all-gather.2.cloned.1.call-update) | async-done | bytes 1048592 | tf_op jit(solution)/shard_map/all_gather | solution.py:56
  68.5 1.3 constant_dynamic-slice_fusion.1
  69.8 1.8 copy.44
  71.6 32.6 %while.17 = (s32[]{:T(128)}, f32[128,32,32]{0,2,1:T(8,128)}, f32[1024,128]{1,0:T(8,128)S(1)}, bf16[2,8,32,128]{3,2,1,0:T(8,128)(2,1)}, bf16[2,128,8,32]{1,3,2,0:...) while((s32[]{:T(128)}, f32[128,32,32]{0,2,1:T(8,128)}, ...), condition=%wide.region_3.4_spmd.clone, body=%wide.region_2.3_spmd.clone.sunk | while | flops 404193280 | bytes 15928666 | solution.py:106
  71.6 1.2 dynamic_slice.46
  74.8 1.7 fusion.79
  76.5 2.2 reshape.95
  78.7 0.9 constant_dynamic-slice_fusion.3
  79.5 0.5 convolution_add_fusion.4
  80.0 0.8 copy-done.2
  80.8 0.3 convolution_convert_fusion.4
  81.1 1.6 reshape.94
  82.7 1.5 fusion.78
  84.3 0.3 fusion.80
  84.6 0.6 copy-done.17
  85.2 2.1 fusion.81
  87.4 1.2 dynamic_slice.46
  90.6 1.7 fusion.79
  92.2 2.2 reshape.95
  94.5 0.9 constant_dynamic-slice_fusion.3
  95.3 0.5 convolution_add_fusion.4
  95.8 0.8 copy-done.2
  96.6 0.3 convolution_convert_fusion.4
  96.9 1.6 reshape.94
  98.5 2.6 fusion.78
  101.1 0.3 fusion.80
  101.4 0.6 copy-done.17
  102.1 2.1 fusion.81
  104.2 1.8 convert_element_type.67
  106.1 2.1 copy.45
  108.3 0.6 convert_reduce_fusion.1
  108.9 51.2 %all-reduce.7.cloned.1.call-done = bf16[128,32,32]{0,2,1:T(8,128)(2,1)} async-done(((bf16[128,32,32]{0,2,1:T(8,128)(2,1)}), bf16[128,32,32]{0,2,1:T(8,128)(2,1)}) %all-reduce.7.cloned.1.call-update) | async-done | bytes 262160 | tf_op jit(solution)/shard_map/psum | solution.py:114
  160.1 1.6 fusion.28
  161.8 21.9 %reduce-scatter.4.cloned.1.call-done = bf16[32,16,32]{2,1,0:T(8,128)(2,1)} async-done(((bf16[128,16,32]{2,1,0:T(8,128)(2,1)}), bf16[32,16,32]{2,1,0:T(8,128)(2,1)}) %reduce-scatter.4.cloned.1.call-update) | async-done | bytes 32784 | tf_op jit(solution)/shard_map/reduce_scatter | solution.py:111
  183.7 1.1 fusion.29
  184.8 1.7 convolution_bitcast_fusion.3
  186.5 32.9 %all-reduce.9.cloned.1.call-done = bf16[128,16,32]{0,2,1:T(8,128)(2,1)} async-done(((bf16[128,16,32]{0,2,1:T(8,128)(2,1)}), bf16[128,16,32]{0,2,1:T(8,128)(2,1)}) %all-reduce.9.cloned.1.call-update) | async-done | bytes 131088 | tf_op jit(solution)/shard_map/psum | solution.py:9
  219.4 1.0 convert_convert_fusion
  220.4 0.2 copy.46
  220.5 0.8 convolution_bitcast_fusion.2
  221.4 0.3 multiply_reduce_fusion
  221.7 0.8 fusion.26
  222.5 51.4 %all-reduce.11.cloned.1.call-done = (f32[256,32]{0,1:T(8,128)}, f32[256,32]{0,1:T(8,128)}, f32[256]{0:T(256)}, f32[128]{0:T(128)}) async-done(((f32[256,32]{0,1:T(8,128)}, f32[256,32]{0,1:T(8,128)}, f32[256]{0:T(256)}, f32[128]{0:T(128)}), (f32[256,32]{0,1:T(8,128)}, f32[256,32]{0,1:T(8,128)}, f32[256]{0:T(256)}, f32[128]{0:T(128)})) %all-reduce.11.cloned.1.call-update) | async-done | bytes 67088 | tf_op jit(solution)/shard_map/psum | solution.py:156
  274.0 0.7 convert_element_type.73
  274.9 1.0 fusion.25
  276.0 36.1 %all-reduce.13.cloned.1.call-done = (f32[256,32]{0,1:T(8,128)}, f32[256,32]{0,1:T(8,128)}, f32[256]{0:T(256)}, f32[128]{0:T(128)}) async-done(((f32[256,32]{0,1:T(8,128)}, f32[256,32]{0,1:T(8,128)}, f32[256]{0:T(256)}, f32[128]{0:T(128)}), (f32[256,32]{0,1:T(8,128)}, f32[256,32]{0,1:T(8,128)}, f32[256]{0:T(256)}, f32[128]{0:T(128)})) %all-reduce.13.cloned.1.call-update) | async-done | bytes 67088 | tf_op jit(solution)/shard_map/psum | solution.py:155
  312.1 1.2 broadcast_multiply_fusion.6
  313.4 1.4 broadcast_multiply_fusion
  314.8 34.1 %reduce-scatter.6.cloned.1.call-done = bf16[128,128]{1,0:T(8,128)(2,1)} async-done(((bf16[1024,128]{1,0:T(8,128)(2,1)}), bf16[128,128]{1,0:T(8,128)(2,1)}) %reduce-scatter.6.cloned.1.call-update) | async-done | bytes 32784 | tf_op jit(solution)/shard_map/reduce_scatter | solution.py:158
  348.9 1.4 convert_element_type.74
  350.3 1.1 broadcast_multiply_fusion.7
  351.4 19.0 %reduce-scatter.8.cloned.1.call-done = f32[32,128]{1,0:T(8,128)} async-done(((f32[128,128]{1,0:T(8,128)}), f32[32,128]{1,0:T(8,128)}) %reduce-scatter.8.cloned.1.call-update) | async-done | bytes 16400 | tf_op jit(solution)/shard_map/reduce_scatter | solution.py:161
  370.4 1.3 broadcast_multiply_fusion.2
  (69 shorter events, 0.7 us)
Async XLA Ops:
  7.2 3.6 copy-start
  7.2 22.1 %copy-start.12 = (bf16[256,32]{0,1:T(8,128)(2,1)S(1)}, bf16[256,32]{0,1:T(8,128)(2,1)}, u32[]{:S(2)}) copy-start(bf16[256,32]{0,1:T(8,128)(2,1)} %param.11) | copy-start | bytes 49156
  7.2 61.3 %all-gather.2.cloned.1.call-start = ((), (), s32[]{:S(2)}) async-start(), calls=%async_computation.3 | async-start | bytes 4718592 | tf_op jit(solution)/shard_map/all_gather | solution.py:56
  8.3 2.4 copy-start.8
  9.6 1.2 copy-start.10
  10.8 18.8 %copy-start.5 = (bf16[32,16,256]{2,1,0:T(8,128)(2,1)}, bf16[32,16,256]{2,1,0:T(8,128)(2,1)S(1)}, u32[]{:S(2)}) copy-start(bf16[32,16,256]{2,1,0:T(8,128)(2,1)S(1)} %fusion.21) | copy-start | bytes 786436
  29.1 131.0 %all-reduce.7.cloned.1.call-start = ((), (), s32[]{:S(2)}) async-start(), calls=%async_computation.5 | async-start | bytes 524288 | tf_op jit(solution)/shard_map/psum | solution.py:114
  45.9 25.7 %copy-start.1 = (bf16[1024,128]{1,0:T(8,128)(2,1)S(1)}, bf16[1024,128]{1,0:T(8,128)(2,1)}, u32[]{:S(2)}) copy-start(bf16[1024,128]{1,0:T(8,128)(2,1)} %param.13) | copy-start | bytes 786436
  80.0 0.8 copy-start.2
  82.7 1.6 copy-start.15
  82.7 1.8 copy-start.16
  84.3 3.1 copy-start.3
  84.6 0.7 copy-start.17
  95.8 0.8 copy-start.2
  98.5 2.6 copy-start.15
  98.5 2.9 copy-start.16
  101.1 3.1 copy-start.3
  101.4 0.7 copy-start.17
  104.2 4.1 %copy-start.7 = (bf16[16,32,128]{2,1,0:T(8,128)(2,1)S(1)}, bf16[16,32,128]{2,1,0:T(8,128)(2,1)}, u32[]{:S(2)}) copy-start(bf16[16,32,128]{2,1,0:T(8,128)(2,1)} %get-tuple-element.311) | copy-start | bytes 393220
  104.2 79.5 %copy-start.13 = (bf16[256,32]{0,1:T(8,128)(2,1)S(1)}, bf16[256,32]{0,1:T(8,128)(2,1)}, u32[]{:S(2)}) copy-start(bf16[256,32]{0,1:T(8,128)(2,1)} %param.11) | copy-start | bytes 49156
  104.2 80.6 %copy-start.6 = (bf16[32,16,256]{2,1,0:T(8,128)(2,1)S(1)}, bf16[32,16,256]{2,1,0:T(8,128)(2,1)}, u32[]{:S(2)}) copy-start(bf16[32,16,256]{2,1,0:T(8,128)(2,1)} %copy-done.5) | copy-start | bytes 786436
  106.1 115.3 %copy-start.14 = (f32[256]{0:T(256)S(1)}, f32[256]{0:T(256)}, u32[]{:S(2)}) copy-start(f32[256]{0:T(256)} %param.10) | copy-start | bytes 3076
  106.1 77.6 %reduce-scatter.4.cloned.1.call-start = ((), (), s32[]{:S(2)}) async-start(), calls=%async_computation.4 | async-start | bytes 655360 | tf_op jit(solution)/shard_map/reduce_scatter | solution.py:111
  108.2 113.4 %copy-start.4 = (bf16[32,16,256]{2,1,0:T(8,128)(2,1)S(1)}, bf16[32,16,256]{2,1,0:T(8,128)(2,1)}, u32[]{:S(2)}) copy-start(bf16[32,16,256]{2,1,0:T(8,128)(2,1)} %param.9) | copy-start | bytes 786436
  108.2 113.5 %copy-start.9 = (f32[32,16]{1,0:T(8,128)S(1)}, f32[32,16]{1,0:T(8,128)}, u32[]{:S(2)}) copy-start(f32[32,16]{1,0:T(8,128)} %copy-done.8) | copy-start | bytes 6148
  108.2 113.5 %copy-start.11 = (f32[32,16]{1,0:T(8,128)S(1)}, f32[32,16]{1,0:T(8,128)}, u32[]{:S(2)}) copy-start(f32[32,16]{1,0:T(8,128)} %copy-done.10) | copy-start | bytes 6148
  108.2 111.1 %all-reduce.9.cloned.1.call-start = ((), (), s32[]{:S(2)}) async-start(), calls=%async_computation.6 | async-start | bytes 262144 | tf_op jit(solution)/shard_map/psum | solution.py:9
  161.7 112.2 %all-reduce.11.cloned.1.call-start = ((), (), s32[]{:S(2)}) async-start(), calls=%async_computation.9 | async-start | bytes 134144 | tf_op jit(solution)/shard_map/psum | solution.py:156
  222.5 89.6 %all-reduce.13.cloned.1.call-start = ((), (), s32[]{:S(2)}) async-start(), calls=%async_computation.10 | async-start | bytes 134144 | tf_op jit(solution)/shard_map/psum | solution.py:155
  274.0 74.9 %reduce-scatter.6.cloned.1.call-start = ((), (), s32[]{:S(2)}) async-start(), calls=%async_computation.7 | async-start | bytes 294912 | tf_op jit(solution)/shard_map/reduce_scatter | solution.py:158
  274.8 95.6 %reduce-scatter.8.cloned.1.call-start = ((), (), s32[]{:S(2)}) async-start(), calls=%async_computation.8 | async-start | bytes 81920 | tf_op jit(solution)/shard_map/reduce_scatter | solution.py:161
Sparse Core Ops, SparseCore 0:
  29.3 39.2 all-gather.1
  106.2 53.8 all-reduce.6
  162.4 21.2 reduce-scatter.3
  186.4 32.8 all-reduce.8
  223.3 50.6 all-reduce.10
  276.4 35.6 all-reduce.12
  315.2 33.6 reduce-scatter.5
  351.1 19.2 reduce-scatter.7
